TPU v7x, 256 devices: a whole 4x4x8 slice. The times are simulated.
256 devices in a mesh: seq: 64 (over x, z_hi, y, core), head: 4 (over z_lo).
Axes of the slice: x: 4, y: 4, z: 8 (z_hi: 2, z_lo: 4; z = z_hi * 4 + z_lo), core: 2. Of those that a mesh axis runs over, the one named last changes fastest.
Arguments:
- span_order: int32 [128], replicated, may hold values from 0 to 127, each once
- queries: bfloat16 [8192, 36864], P('seq', 'head'), may hold values from -32 to 32
- latent_kv: bfloat16 [8192, 576], P(('seq', 'head')), may hold values from -8 to 8
- w_uv: bfloat16 [64, 512, 128], P('head'), may hold values from -0.25 to 0.25
Outputs:
- attended: bfloat16 [8192, 8192], P('seq', 'head')
Inputs may be any that keep to these rules, and one draw needn't show every extreme that they name: `span_order`: each of 0 to 127 appears once.
All inputs are finite; a program needn't handle non-finite values.
Results may differ from a plain program's by a relative error of at most 0.0065.
Values may be sent and summed in bfloat16 or wider, within the bound.
No kernel may reach another device: no remote copies, remote signals or barrier semaphores. Data moves between devices by JAX's collectives and lax.ppermute only.
A program may use at most 128 MiB of HBM per device.

v0:
```python
import math
import jax
import jax.numpy as jnp
from jax import lax
from jax.sharding import PartitionSpec as P

ROPE_DIM = 64
NOPE_DIM = 128
SEQS = 2
theta_base = 10000.0
floor_score = -1e30


def copy_for_each(shard, axis):
    copies = jnp.broadcast_to(shard, (lax.axis_size(axis), *shard.shape))
    return lax.all_to_all(copies, axis, split_axis=0, concat_axis=0, tiled=True)


def joined_along(tiles, dim):
    tiles = jnp.moveaxis(tiles, 0, dim)
    shape = tiles.shape
    return tiles.reshape(*shape[:dim], shape[dim] * shape[dim + 1], *shape[dim + 2 :])


def collect(shard, axis, dim):
    tiles = copy_for_each(shard, axis)
    return joined_along(tiles, dim)


def angle_tables(positions, half_width):
    inverse_freq = jnp.exp(
        -math.log(theta_base) * jnp.arange(half_width, dtype=jnp.float32) / half_width
    )
    phases = positions.astype(jnp.float32)[:, None] * inverse_freq[None, :]
    return (jnp.cos(phases), jnp.sin(phases))


def rotate(values, cosine, sine_table):
    half_width = values.shape[-1] // 2
    lower_part = values[..., :half_width]
    upper_part = values[..., half_width:]
    return jnp.concatenate(
        [
            lower_part * cosine - upper_part * sine_table,
            upper_part * cosine + lower_part * sine_table,
        ],
        -1,
    )


def unchanged(running):
    return running


def per_device(span_order, queries, latent_kv, w_uv):
    tok_dev = queries.shape[0]
    head_count = w_uv.shape[0]
    latent_rank = w_uv.shape[1]
    row_width = queries.shape[1] // head_count
    rope_width = row_width - latent_rank
    n_seq = lax.axis_size("seq")
    n_head = lax.axis_size("head")
    span_len = tok_dev // 2
    seq_len = tok_dev * n_seq // SEQS
    stream_ids = (
        span_order[:, None] * span_len + jnp.arange(span_len, dtype=jnp.int32)[None, :]
    ).reshape(-1)
    seq_of = stream_ids // seq_len
    pos_of = stream_ids % seq_len
    kv_count = latent_kv.shape[0]
    kv_first = (lax.axis_index("seq") * n_head + lax.axis_index("head")) * kv_count
    kv_pos = lax.dynamic_slice_in_dim(pos_of, kv_first, kv_count)
    cos_keys, sin_keys = angle_tables(kv_pos, rope_width // 2)
    key_rows = jnp.concatenate(
        [
            latent_kv[:, :latent_rank],
            rotate(latent_kv[:, latent_rank:].astype(jnp.float32), cos_keys, sin_keys).astype(
                jnp.bfloat16
            ),
        ],
        1,
    )
    query_first = lax.axis_index("seq") * tok_dev
    query_pos = lax.dynamic_slice_in_dim(pos_of, query_first, tok_dev)
    query_seq = lax.dynamic_slice_in_dim(seq_of, query_first, tok_dev)
    cos_query, sin_query = angle_tables(query_pos, rope_width // 2)
    query_grid = queries.reshape(tok_dev, head_count, row_width)
    rotated = rotate(
        query_grid[..., latent_rank:].astype(jnp.float32),
        cos_query[:, None, :],
        sin_query[:, None, :],
    ).astype(jnp.bfloat16)
    query_grid = jnp.concatenate([query_grid[..., :latent_rank], rotated], -1)
    query_blocks = (
        query_grid.reshape(2, span_len, head_count, row_width)
        .transpose(0, 2, 1, 3)
        .reshape(2, head_count * span_len, row_width)
    )
    span_pos = query_pos.reshape(2, span_len)
    span_seq = query_seq.reshape(2, span_len)[:, 0]
    logit_scale_factor = (NOPE_DIM + ROPE_DIM) ** (-0.5)
    group_rows = collect(key_rows, "head", 0)
    shard_rows = lax.all_gather(group_rows, "seq", axis=0, tiled=True)
    row_count = shard_rows.shape[0]
    maxima = jnp.full((2, head_count * span_len), floor_score, jnp.float32)
    totals = jnp.zeros((2, head_count * span_len), jnp.float32)
    weighted_sums = jnp.zeros((2, head_count * span_len, latent_rank), jnp.float32)
    new_maxima = []
    new_totals = []
    new_sums = []
    for half_index in range(2):
        visible = (seq_of[None, :] == span_seq[half_index]) & (
            pos_of[None, :] <= span_pos[half_index][:, None]
        )
        block_rows = query_blocks[half_index]

        def update(state_now, visible=visible, block_rows=block_rows):
            old_top, old_total, old_sum = state_now
            logit_scores = (
                lax.dot_general(
                    block_rows,
                    shard_rows,
                    (((1,), (1,)), ((), ())),
                    preferred_element_type=jnp.float32,
                )
                * logit_scale_factor
            )
            logit_scores = jnp.where(
                visible[None], logit_scores.reshape(head_count, span_len, row_count), -jnp.inf
            ).reshape(head_count * span_len, row_count)
            new_top = jnp.maximum(old_top, jnp.max(logit_scores, 1))
            expo = jnp.exp(logit_scores - new_top[:, None])
            new_total = jnp.sum(expo, 1)
            contrib = jnp.dot(
                expo.astype(jnp.bfloat16),
                shard_rows[:, :latent_rank],
                preferred_element_type=jnp.float32,
            )
            return (new_top, new_total, contrib)

        state_now = (maxima[half_index], totals[half_index], weighted_sums[half_index])
        state_now = lax.cond(jnp.any(visible), update, unchanged, state_now)
        new_maxima.append(state_now[0])
        new_totals.append(state_now[1])
        new_sums.append(state_now[2])
    running = (jnp.stack(new_maxima), jnp.stack(new_totals), jnp.stack(new_sums))
    maxima, totals, weighted_sums = running
    latent_out = (weighted_sums / totals[..., None]).astype(jnp.bfloat16)
    latent_out = latent_out.reshape(2, head_count, span_len, latent_rank)
    projected = jnp.einsum(
        "shcr,hrv->shcv", latent_out, w_uv, preferred_element_type=jnp.float32
    ).astype(jnp.bfloat16)
    return projected.transpose(0, 2, 1, 3).reshape(tok_dev, head_count * w_uv.shape[2])


def solution(mesh):
    in_specs = (P(), P("seq", "head"), P(("seq", "head"), None), P("head", None, None))
    out_specs = P("seq", "head")
    return jax.shard_map(
        per_device, mesh=mesh, in_specs=in_specs, out_specs=out_specs, check_vma=False
    )
```

profile of v0, /device:TPU:1, one launch (start us, length us, event | category | flops | bytes accessed | tf_op | source)
XLA Modules:
  0.0 265.8 jit_solution(6816313810189963737)
XLA Ops:
  6.5 0.0 copy-start
  6.5 0.0 all-gather.2.cloned.1.call-start
  6.5 0.8 slice_convert_fusion.1
  7.4 0.8 slice.65
  8.2 0.7 broadcast_multiply_fusion
  8.8 0.1 iota_add_fusion
  8.9 0.1 add.64
  9.0 0.1 dynamic-slice_convert_fusion
  9.1 0.1 fusion.31
  9.2 0.1 pad_maximum_fusion.1
  9.4 12.0 %all_to_all.5 = bf16[4,32,576]{2,1,0:T(8,128)(2,1)} all-to-all(bf16[4,32,576]{2,1,0:T(8,128)(2,1)S(1)} %broadcast_in_dim.44), channel_id=1, replica_groups=mesh['seq'=64,'head'=4] {'head'}, dimensions={0} | all-to-all | bytes 294912 | tf_op jit(solution)/shard_map/all_to_all | solution.py:16
  21.4 0.0 all-gather.2.cloned.1.call-update
  21.4 0.1 dynamic_slice.9
  21.5 0.1 reshape.165
  21.5 0.1 fusion.36
  21.6 0.5 fusion.37
  22.1 0.1 fusion.38
  22.2 1.3 broadcast_compare_fusion
  23.5 2.6 fusion.34
  27.3 4.3 %copy.6 = bf16[128,9216]{0,1:T(8,128)(2,1)} copy(bf16[128,9216]{1,0:T(8,128)(2,1)} %param.9) | data formatting | bytes 4718592 | tf_op args[1]
  31.6 1.7 slice.73
  33.4 0.1 multiply_cosine_fusion.1
  33.5 1.0 slice_convert_fusion
  34.5 0.1 subtract_convert_fusion
  34.6 1.6 pad_maximum_fusion
  36.2 4.9 %copy.7 = bf16[128,16,576]{2,1,0:T(8,128)(2,1)} copy(bf16[128,16,576]{0,2,1:T(8,128)(2,1)} %pad_maximum_fusion) | data formatting | bytes 4718592 | tf_op jit(solution)/shard_map/concatenate | solution.py:93
  41.1 105.8 %all-gather.2.cloned.1.call-done = bf16[8192,576]{1,0:T(8,128)(2,1)} async-done(((bf16[128,576]{1,0:T(8,128)(2,1)}), bf16[8192,576]{1,0:T(8,128)(2,1)}) %all-gather.2.cloned.1.call-update) | async-done | bytes 9437200 | tf_op jit(solution)/shard_map/all_gather | solution.py:103
  146.9 53.9 %conditional.2 = (f32[1,1024]{1,0:T(1,128)S(1)}, f32[1,16,64,512]{3,2,1,0:T(8,128)}) conditional(s32[]{:T(128)} %convert_element_type.37, () %tuple.29, (pred[64,8192]{1,0:T(8,128)(4,1)}, bf16[2,16,64,576]{3,1,2,0:T(8,128)(2,1)}, bf16[8192,576]{1,0:T(8,128)(2,1)}) %tuple.56), branch_computations={%region_1.2_spmd, %region_2.5_spmd} | conditional | flops 18320719872 | bytes 129912848 | solution.py:142
  146.9 2.3 copy.8
  149.2 0.1 slice.71
  149.3 22.3 %fusion = (f32[1024]{0:T(1024)S(1)}, f32[1024,8192]{1,0:T(8,128)}) fusion(pred[64,8192]{1,0:T(8,128)(4,1)} %get-tuple-element.25, bf16[1024,576]{1,0:T(8,128)(2,1)S(1)} %bitcast.59, bf16[8192,576]{1,0:T(8,128)(2,1)} %get-tuple-element.27), kind=kOutput, calls=%fused_computation.2 | convolution fusion | flops 9688841216 | bytes 44699648 | tf_op jit(solution)/shard_map/cond/branch_1_fun/dot_general | solution.py:120
  171.6 16.7 %fusion.1 = (bf16[1024,8192]{1,0:T(8,128)(2,1)S(1)}, f32[1024]{0:T(1024)S(1)}) fusion(f32[1024,8192]{1,0:T(8,128)} %get-tuple-element.52, f32[1024]{0:T(1024)S(1)} %broadcast_maximum_fusion, pred[64,8192]{1,0:T(8,128)(4,1)} %get-tuple-element.25), kind=kLoop, calls=%fused_computation.3 | loop fusion | flops 41942016 | bytes 50864128 | tf_op jit(solution)/shard_map/cond/branch_1_fun/convert_element_type | solution.py:135
  188.4 12.3 %fusion.3 = f32[1024,512]{1,0:T(8,128)} fusion(bf16[1024,8192]{1,0:T(8,128)(2,1)S(1)} %get-tuple-element.49, bf16[8192,576]{1,0:T(8,128)(2,1)} %get-tuple-element.27), kind=kOutput, calls=%fused_computation.5 | convolution fusion | flops 8589934592 | bytes 27262976 | tf_op jit(solution)/shard_map/cond/branch_1_fun/dot_general | solution.py:134
  200.7 53.9 %conditional.3 = (f32[1,1024]{1,0:T(1,128)S(1)}, f32[1,16,64,512]{3,2,1,0:T(8,128)}) conditional(s32[]{:T(128)} %convert_element_type.42, () %tuple.31, (pred[64,8192]{1,0:T(8,128)(4,1)}, bf16[2,16,64,576]{3,1,2,0:T(8,128)(2,1)}, bf16[8192,576]{1,0:T(8,128)(2,1)}) %tuple.57), branch_computations={%region_6.7_spmd, %region_7.10_spmd} | conditional | flops 18320719872 | bytes 129912848 | solution.py:142
  200.7 2.3 copy.9
  203.1 0.1 slice.72
  203.2 22.3 %fusion.5 = (f32[1024]{0:T(1024)S(1)}, f32[1024,8192]{1,0:T(8,128)}) fusion(pred[64,8192]{1,0:T(8,128)(4,1)} %get-tuple-element.28, bf16[1024,576]{1,0:T(8,128)(2,1)S(1)} %bitcast.60, bf16[8192,576]{1,0:T(8,128)(2,1)} %get-tuple-element.30), kind=kOutput, calls=%fused_computation.10 | convolution fusion | flops 9688841216 | bytes 44699648 | tf_op jit(solution)/shard_map/cond/branch_1_fun/dot_general | solution.py:120
  225.5 16.7 %fusion.6 = (bf16[1024,8192]{1,0:T(8,128)(2,1)S(1)}, f32[1024]{0:T(1024)S(1)}) fusion(f32[1024,8192]{1,0:T(8,128)} %get-tuple-element.56, f32[1024]{0:T(1024)S(1)} %broadcast_maximum_fusion.1, pred[64,8192]{1,0:T(8,128)(4,1)} %get-tuple-element.28), kind=kLoop, calls=%fused_computation.11 | loop fusion | flops 41942016 | bytes 50864128 | tf_op jit(solution)/shard_map/cond/branch_1_fun/convert_element_type | solution.py:135
  242.2 12.3 %fusion.8 = f32[1024,512]{1,0:T(8,128)} fusion(bf16[1024,8192]{1,0:T(8,128)(2,1)S(1)} %get-tuple-element.53, bf16[8192,576]{1,0:T(8,128)(2,1)} %get-tuple-element.30), kind=kOutput, calls=%fused_computation.13 | convolution fusion | flops 8589934592 | bytes 27262976 | tf_op jit(solution)/shard_map/cond/branch_1_fun/dot_general | solution.py:134
  254.6 0.1 div.37
  254.7 0.0 copy-done
  254.7 3.0 %fusion.19 = bf16[2,64,16,128]{3,1,0,2:T(8,128)(2,1)S(1)} fusion(bf16[16,512,128]{2,1,0:T(8,128)(2,1)S(1)} %copy-done, f32[1,16,64,512]{3,2,1,0:T(8,128)} %get-tuple-element.36, f32[1,16,64,512]{3,2,1,0:T(8,128)} %get-tuple-element.35, f32[2,16,64]{2,1,0:T(8,128)S(1)} %div.37), kind=kOutput, calls=%fused_computation.25 | convolution fusion | flops 271843328 | bytes 6823936 | tf_op jit(solution)/shard_map/shcr,hrv->shcv/dot_general | solution.py:150
  257.7 0.3 copy.11
  258.0 0.9 copy.21
  (6 shorter events, 0.1 us)
Async XLA Ops:
  6.5 248.1 %copy-start = (bf16[16,512,128]{2,1,0:T(8,128)(2,1)S(1)}, bf16[16,512,128]{2,1,0:T(8,128)(2,1)}, u32[]{:S(2)}) copy-start(bf16[16,512,128]{2,1,0:T(8,128)(2,1)} %param.11) | copy-start | bytes 6291460
  6.5 140.3 %all-gather.2.cloned.1.call-start = ((), (), s32[]{:S(2)}) async-start(), calls=%async_computation.1 | async-start | bytes 10649600 | tf_op jit(solution)/shard_map/all_gather | solution.py:103
Sparse Core Ops, SparseCore 0:
  21.5 125.3 all-gather.1
where the time goes:
time: 266 us
  waiting for transfers between devices  106 us (40%)
  matrix products  72.3 us (27%)
  other arithmetic  42.1 us (16%)
  local copies, waits for them, and re-layouts  18.8 us (7%)
  between operations  14.7 us (6%)
  blocking collectives  12 us (5%)
    all_gather x1, waiting for transfers between devices, per_device(): shard_rows = lax.all_gather(group_rows, 'seq', axis=0, tiled=True)  106 us
    dot_general x2, matrix products, update(): lax.dot_general(block_rows, shard_rows, (((1,), (1,)), ((), ())), preferr...  44.6 us
    convert_element_type x2, other arithmetic, update(): expo.astype(jnp.bfloat16)  33.5 us
    dot_general x2, matrix products, update(): jnp.dot(expo.astype(jnp.bfloat16), shard_rows[:, :latent_rank], preferred...  24.7 us
    all_to_all x1, blocking collectives, copy_for_each(): return lax.all_to_all(copies, axis, split_axis=0, concat_axis=0, tiled=True)  12 us
  transfers between devices with their start and end apart: 1, of which 1 were waited for; matrix products, arithmetic and copies ran while one was open for 7% of the time, Pallas kernels for 0%

commit v1 on v0

--- a/solution.py
+++ b/solution.py
@@ -100,7 +100,8 @@
     span_seq = query_seq.reshape(2, span_len)[:, 0]
     logit_scale_factor = (NOPE_DIM + ROPE_DIM) ** (-0.5)
     group_rows = collect(key_rows, "head", 0)
-    shard_rows = lax.all_gather(group_rows, "seq", axis=0, tiled=True)
+    outgoing = jnp.stack([group_rows] * lax.axis_size("seq"))
+    shard_rows = jnp.concatenate(lax.all_to_all(outgoing, "seq", 0, 0), axis=0)
     row_count = shard_rows.shape[0]
     maxima = jnp.full((2, head_count * span_len), floor_score, jnp.float32)
     totals = jnp.zeros((2, head_count * span_len), jnp.float32)

time: 266 us -> 414 us (1.56)
  waiting for transfers between devices: 106 us -> 191 us
  local copies, waits for them, and re-layouts: 18.8 us -> 61.7 us
  starting transfers between devices: 0.01 us -> 13.8 us
  between operations: 14.7 us -> 1.38 us
  other arithmetic: 42.1 us -> 52.5 us
  matrix products: 72.3 us -> 79.6 us
    all_to_all x0 -> x1, waiting for transfers between devices: none -> 191 us  [per_device(): shard_rows = jnp.concatenate(lax.all_to_all(outgoing, 'seq', 0, 0), axis=0)]
    all_gather x1 -> x0, waiting for transfers between devices: 106 us -> none  [per_device(): shard_rows = lax.all_gather(group_rows, 'seq', axis=0, tiled=True)]
    another operation x2 -> x6, local copies, waits for them, and re-layouts: 4.69 us -> 38.9 us
    all_to_all x0 -> x1, starting transfers between devices: none -> 13.8 us  [per_device(): shard_rows = jnp.concatenate(lax.all_to_all(outgoing, 'seq', 0, 0), axis=0)]
    convert_element_type x2, other arithmetic: 33.5 us -> 44.4 us  [update(): expo.astype(jnp.bfloat16)]
    reshape x0 -> x1, local copies, waits for them, and re-layouts: none -> 8.63 us  [per_device(): shard_rows = jnp.concatenate(lax.all_to_all(outgoing, 'seq', 0, 0), axis=0)]
    dot_general x2, matrix products: 24.7 us -> 31.5 us  [update(): jnp.dot(expo.astype(jnp.bfloat16), shard_rows[:, :latent_rank], preferred...]
  transfers between devices with their start and end apart: 1 -> 1, of which waited for: 1 -> 1; matrix products, arithmetic and copies ran while one was open for 7% -> 4% of each run, Pallas kernels for 0% -> 0%
where the time goes in v1:
time: 414 us; the launch traced here: 412 us
  waiting for transfers between devices  191 us (46%)
  matrix products  79.6 us (19%)
  local copies, waits for them, and re-layouts  61.7 us (15%)
  other arithmetic  52.5 us (13%)
  starting transfers between devices  13.8 us (3%)
  blocking collectives  11.9 us (3%)
    all_to_all x1, waiting for transfers between devices, per_device(): shard_rows = jnp.concatenate(lax.all_to_all(outgoing, 'seq', 0, 0), axis=0)  191 us
    dot_general x2, matrix products, update(): lax.dot_general(block_rows, shard_rows, (((1,), (1,)), ((), ())), preferr...  45.2 us
    convert_element_type x2, other arithmetic, update(): expo.astype(jnp.bfloat16)  44.4 us
    another operation x4, local copies, waits for them, and re-layouts  32.8 us
    dot_general x2, matrix products, update(): jnp.dot(expo.astype(jnp.bfloat16), shard_rows[:, :latent_rank], preferred...  31.5 us
    all_to_all x1, starting transfers between devices, per_device(): shard_rows = jnp.concatenate(lax.all_to_all(outgoing, 'seq', 0, 0), axis=0)  13.8 us
    all_to_all x1, blocking collectives, copy_for_each(): return lax.all_to_all(copies, axis, split_axis=0, concat_axis=0, tiled=True)  11.9 us
    reshape x1, local copies, waits for them, and re-layouts, per_device(): shard_rows = jnp.concatenate(lax.all_to_all(outgoing, 'seq', 0, 0), axis=0)  8.63 us
  transfers between devices with their start and end apart: 1, of which 1 were waited for; matrix products, arithmetic and copies ran while one was open for 4% of the time, Pallas kernels for 0%

profile of v1, /device:TPU:1, one launch (start us, length us, event | category | flops | bytes accessed | tf_op | source)
XLA Modules:
  0.0 412.0 jit_solution(5340027363032271295)
XLA Ops:
  0.0 0.0 copy-start
  0.0 0.9 slice_convert_fusion.1
  0.9 0.8 slice.65
  1.6 0.7 broadcast_multiply_fusion
  2.3 0.1 iota_add_fusion
  2.4 0.1 add.64
  2.5 0.1 dynamic-slice_convert_fusion
  2.6 0.1 fusion.31
  2.7 0.1 pad_maximum_fusion.1
  2.8 11.9 %all_to_all.10 = bf16[4,32,576]{2,1,0:T(8,128)(2,1)S(1)} all-to-all(bf16[4,32,576]{2,1,0:T(8,128)(2,1)S(1)} %broadcast_in_dim.44), channel_id=1, replica_groups=mesh['seq'=64,'head'=4] {'head'}, dimensions={0} | all-to-all | bytes 294912 | tf_op jit(solution)/shard_map/all_to_all | solution.py:16
  14.7 0.1 copy.21
  14.9 5.9 %stack.33 = bf16[64,128,576]{1,2,0:T(8,128)(2,1)} broadcast(bf16[128,576]{0,1:T(8,128)(2,1)S(1)} %copy.21), dimensions={1,2} | broadcast | bytes 9584640 | tf_op jit(solution)/shard_map/stack | solution.py:103
  20.8 13.8 %all-to-all-start.1 = ((bf16[64,128,576]{1,2,0:T(8,128)(2,1)}), bf16[64,128,576]{1,2,0:T(8,128)(2,1)}, u32[]{:S(2)}, u32[]{:S(2)}) async-start(bf16[64,128,576]{1,2,0:T(8,128)(2,1)} %stack.33), calls=%async_computation.1 | async-start | bytes 18874368 | tf_op jit(solution)/shard_map/all_to_all | solution.py:104
  34.6 0.1 dynamic_slice.9
  34.7 0.1 reshape.167
  34.8 4.3 %copy.19 = bf16[128,9216]{0,1:T(8,128)(2,1)} copy(bf16[128,9216]{1,0:T(8,128)(2,1)} %param.9) | data formatting | bytes 4718592 | tf_op args[1]
  39.1 1.7 slice.75
  40.8 0.1 fusion.36
  40.9 0.1 multiply_cosine_fusion.1
  41.0 1.0 slice_convert_fusion
  42.0 0.1 subtract_convert_fusion
  42.1 1.6 pad_maximum_fusion
  43.7 4.9 %copy.20 = bf16[128,16,576]{2,1,0:T(8,128)(2,1)} copy(bf16[128,16,576]{0,2,1:T(8,128)(2,1)} %pad_maximum_fusion) | data formatting | bytes 4718592 | tf_op jit(solution)/shard_map/concatenate | solution.py:93
  48.6 0.5 fusion.37
  49.2 0.1 fusion.38
  49.2 1.3 broadcast_compare_fusion
  50.5 2.0 fusion.34
  53.8 191.1 %all-to-all-done.1 = bf16[64,128,576]{1,2,0:T(8,128)(2,1)} async-done(((bf16[64,128,576]{1,2,0:T(8,128)(2,1)}), bf16[64,128,576]{1,2,0:T(8,128)(2,1)}, u32[]{:S(2)}, u32[]{:S(2)}) %all-to-all-start.1) | async-done | bytes 9437216 | tf_op jit(solution)/shard_map/all_to_all | solution.py:104
  244.8 8.6 %copy_bitcast_fusion = bf16[8192,576]{0,1:T(8,128)(2,1)} fusion(bf16[64,128,576]{1,2,0:T(8,128)(2,1)} %all-to-all-done.1), kind=kLoop, calls=%fused_computation.16 | loop fusion | bytes 18874368 | tf_op jit(solution)/shard_map/reshape | solution.py:104
  253.4 77.1 %conditional.2 = (f32[1,1024]{1,0:T(1,128)S(1)}, f32[1,16,64,512]{3,2,1,0:T(8,128)}) conditional(s32[]{:T(128)} %convert_element_type.37, () %tuple.29, (pred[64,8192]{1,0:T(8,128)(4,1)S(1)}, bf16[2,16,64,576]{3,1,2,0:T(8,128)(2,1)}, bf16[8192,576]{0,1:T(8,128)(2,1)}) %tuple.58), branch_computations={%region_1.2_spmd, %region_2.5_spmd} | conditional | flops 18320719872 | bytes 148787216 | solution.py:143
  253.4 2.3 copy.23
  255.8 0.1 slice.71
  255.9 22.6 %fusion = (f32[1024]{0:T(1024)S(1)}, f32[1024,8192]{1,0:T(8,128)}) fusion(pred[64,8192]{1,0:T(8,128)(4,1)S(1)} %get-tuple-element.25, bf16[1024,576]{1,0:T(8,128)(2,1)S(1)} %bitcast.64, bf16[8192,576]{0,1:T(8,128)(2,1)} %get-tuple-element.53), kind=kOutput, calls=%fused_computation.2 | convolution fusion | flops 9688841216 | bytes 44699648 | tf_op jit(solution)/shard_map/cond/branch_1_fun/dot_general | solution.py:121
  278.5 22.2 %fusion.1 = (bf16[1024,8192]{1,0:T(8,128)(2,1)}, f32[1024]{0:T(1024)S(1)}) fusion(f32[1024,8192]{1,0:T(8,128)} %get-tuple-element.64, f32[1024]{0:T(1024)S(1)} %broadcast_maximum_fusion, pred[64,8192]{1,0:T(8,128)(4,1)S(1)} %get-tuple-element.25), kind=kLoop, calls=%fused_computation.3 | loop fusion | flops 41942016 | bytes 50864128 | tf_op jit(solution)/shard_map/cond/branch_1_fun/convert_element_type | solution.py:136
  300.7 14.1 %copy.24 = bf16[8192,576]{1,0:T(8,128)(2,1)} copy(bf16[8192,576]{0,1:T(8,128)(2,1)} %get-tuple-element.53) | data formatting | bytes 18874368 | tf_op jit(solution)/shard_map
  314.8 15.7 %fusion.3 = f32[1024,512]{1,0:T(8,128)} fusion(bf16[1024,8192]{1,0:T(8,128)(2,1)} %get-tuple-element.61, bf16[8192,576]{1,0:T(8,128)(2,1)} %copy.24), kind=kOutput, calls=%fused_computation.5 | convolution fusion | flops 8589934592 | bytes 27262976 | tf_op jit(solution)/shard_map/cond/branch_1_fun/dot_general | solution.py:135
  330.5 77.1 %conditional.3 = (f32[1,1024]{1,0:T(1,128)S(1)}, f32[1,16,64,512]{3,2,1,0:T(8,128)}) conditional(s32[]{:T(128)} %convert_element_type.42, () %tuple.31, (pred[64,8192]{1,0:T(8,128)(4,1)S(1)}, bf16[2,16,64,576]{3,1,2,0:T(8,128)(2,1)}, bf16[8192,576]{0,1:T(8,128)(2,1)}) %tuple.59), branch_computations={%region_6.7_spmd, %region_7.10_spmd} | conditional | flops 18320719872 | bytes 148787216 | solution.py:143
  330.5 2.3 copy.25
  332.9 0.1 slice.73
  333.0 22.6 %fusion.5 = (f32[1024]{0:T(1024)S(1)}, f32[1024,8192]{1,0:T(8,128)}) fusion(pred[64,8192]{1,0:T(8,128)(4,1)S(1)} %get-tuple-element.28, bf16[1024,576]{1,0:T(8,128)(2,1)S(1)} %bitcast.65, bf16[8192,576]{0,1:T(8,128)(2,1)} %get-tuple-element.56), kind=kOutput, calls=%fused_computation.10 | convolution fusion | flops 9688841216 | bytes 44699648 | tf_op jit(solution)/shard_map/cond/branch_1_fun/dot_general | solution.py:121
  355.6 22.2 %fusion.6 = (bf16[1024,8192]{1,0:T(8,128)(2,1)}, f32[1024]{0:T(1024)S(1)}) fusion(f32[1024,8192]{1,0:T(8,128)} %get-tuple-element.68, f32[1024]{0:T(1024)S(1)} %broadcast_maximum_fusion.1, pred[64,8192]{1,0:T(8,128)(4,1)S(1)} %get-tuple-element.28), kind=kLoop, calls=%fused_computation.11 | loop fusion | flops 41942016 | bytes 50864128 | tf_op jit(solution)/shard_map/cond/branch_1_fun/convert_element_type | solution.py:136
  377.8 14.1 %copy.26 = bf16[8192,576]{1,0:T(8,128)(2,1)} copy(bf16[8192,576]{0,1:T(8,128)(2,1)} %get-tuple-element.56) | data formatting | bytes 18874368 | tf_op jit(solution)/shard_map
  391.9 15.7 %fusion.8 = f32[1024,512]{1,0:T(8,128)} fusion(bf16[1024,8192]{1,0:T(8,128)(2,1)} %get-tuple-element.65, bf16[8192,576]{1,0:T(8,128)(2,1)} %copy.26), kind=kOutput, calls=%fused_computation.13 | convolution fusion | flops 8589934592 | bytes 27262976 | tf_op jit(solution)/shard_map/cond/branch_1_fun/dot_general | solution.py:135
  407.6 0.1 div.37
  407.7 0.0 copy-done
  407.7 3.0 fusion.19
  410.7 0.3 copy.28
  411.1 0.9 copy.42
  (6 shorter events, 0.1 us)
Async XLA Ops:
  0.0 407.7 %copy-start = (bf16[16,512,128]{2,1,0:T(8,128)(2,1)S(1)}, bf16[16,512,128]{2,1,0:T(8,128)(2,1)}, u32[]{:S(2)}) copy-start(bf16[16,512,128]{2,1,0:T(8,128)(2,1)} %param.11) | copy-start | bytes 6291460
  20.8 224.0 %all-to-all-start.1 = ((bf16[64,128,576]{1,2,0:T(8,128)(2,1)}), bf16[64,128,576]{1,2,0:T(8,128)(2,1)}, u32[]{:S(2)}, u32[]{:S(2)}) async-start(bf16[64,128,576]{1,2,0:T(8,128)(2,1)} %stack.33), calls=%async_computation.1 | async-start | bytes 18874368 | tf_op jit(solution)/shard_map/all_to_all | solution.py:104
